TPU v7x, 32 devices: a whole 2x2x4 slice. The times are simulated.
32 devices in a mesh: row: 8 (over y, x, core), col: 4 (over z).
Axes of the slice: x: 2, y: 2, z: 4, core: 2. Of those that a mesh axis runs over, the one named last changes fastest.
Arguments:
- query_proj: bfloat16 [192, 192, 128], P('row', 'col'), may hold values from -8 to 8
- key_proj: bfloat16 [192, 192, 128], P('row', 'col'), may hold values from -8 to 8
- value_proj: bfloat16 [192, 192, 128], P('row', 'col'), may hold values from -6 to 6
- pair_bias: bfloat16 [4, 192, 192], P(None, 'col', 'row'), may hold values from -9 to 9
- pair_mask: int32 [192, 192], P('row', 'col'), may hold values 0 or 1
- grad_out: bfloat16 [192, 192, 128], P('row', 'col'), may hold values from -18 to 18
Outputs:
- grad_query: bfloat16 [192, 192, 128], P('row', 'col')
- grad_key: bfloat16 [192, 192, 128], P('row', 'col')
- grad_value: bfloat16 [192, 192, 128], P('row', 'col')
- grad_bias: float32 [4, 192, 192], P(None, 'col', 'row')
All inputs are finite; a program needn't handle non-finite values. No bound on the sum of `pair_mask` on one device may be relied on, other than what follows from the above.
Results may differ from a plain program's by a relative error of at most 0.0096.
Values may be sent and summed in bfloat16 or wider, within the bound.
A program may use at most 128 MiB of HBM per device.

v0:
```python
import math

import jax
import jax.numpy as jnp
from jax import lax
from jax.sharding import PartitionSpec as P

HEADS = 4
HEAD_DIM = 32


def block_grads(queries, keys_all, values_all, grads, mask_all, bias_full):
    block_rows, query_count, channel_count = queries.shape
    key_count = keys_all.shape[1]
    scale = 1.0 / math.sqrt(HEAD_DIM)
    query_heads = queries.reshape(block_rows, query_count, HEADS, HEAD_DIM)
    key_heads = keys_all.reshape(block_rows, key_count, HEADS, HEAD_DIM)
    value_heads = values_all.reshape(block_rows, key_count, HEADS, HEAD_DIM)
    grad_heads = grads.reshape(block_rows, query_count, HEADS, HEAD_DIM)
    masked = 1000000000.0 * (mask_all.astype(jnp.float32) - 1.0)
    scores = (
        jnp.einsum("bjhd,bkhd->bhjk", query_heads, key_heads, preferred_element_type=jnp.float32)
        * scale
    )
    scores = scores + bias_full.astype(jnp.float32)[None] + masked[:, None, None, :]
    top_score = jnp.max(scores, axis=-1, keepdims=True)
    weights = jnp.exp(scores - top_score)
    attn_probs = weights / jnp.sum(weights, axis=-1, keepdims=True)
    attn_low = attn_probs.astype(jnp.bfloat16)
    attended = jnp.einsum(
        "bhjk,bkhd->bjhd", attn_low, value_heads, preferred_element_type=jnp.float32
    )
    row_delta = jnp.sum(grad_heads.astype(jnp.float32) * attended, axis=-1)
    grad_probs = jnp.einsum(
        "bjhd,bkhd->bhjk", grad_heads, value_heads, preferred_element_type=jnp.float32
    )
    grad_scores = attn_probs * (grad_probs - jnp.transpose(row_delta, (0, 2, 1))[..., None])
    scores_low = grad_scores.astype(jnp.bfloat16)
    grad_queries = (
        jnp.einsum("bhjk,bkhd->bjhd", scores_low, key_heads, preferred_element_type=jnp.float32)
        * scale
    )
    grad_keys = (
        jnp.einsum("bhjk,bjhd->bkhd", scores_low, query_heads, preferred_element_type=jnp.float32)
        * scale
    )
    grad_values = jnp.einsum(
        "bhjk,bjhd->bkhd", attn_low, grad_heads, preferred_element_type=jnp.float32
    )
    bias_grad = jnp.sum(grad_scores, axis=0)
    return (
        grad_queries.reshape(block_rows, query_count, channel_count),
        grad_keys.reshape(block_rows, key_count, channel_count),
        grad_values.reshape(block_rows, key_count, channel_count),
        bias_grad,
    )


def all_blocks(queries, keys_all, values_all, grads, mask_all, bias_full):
    row_count, query_count, channel_count = queries.shape
    key_count = keys_all.shape[1]
    block_rows = 1
    while (
        block_rows * 2 <= row_count
        and row_count % (block_rows * 2) == 0
        and (block_rows * query_count < 512)
    ):
        block_rows = block_rows * 2
    steps_count = row_count // block_rows

    def split_rows(array):
        return array.reshape((steps_count, block_rows) + array.shape[1:])

    def one_block(bias_sum, pieces):
        grad_queries, grad_keys, grad_values, bias_grad = block_grads(
            pieces[0], pieces[1], pieces[2], pieces[3], pieces[4], bias_full
        )
        return (bias_sum + bias_grad, (grad_queries, grad_keys, grad_values))

    start_sum = jnp.zeros((HEADS, query_count, key_count), jnp.float32)
    bias_sum, stacked = lax.scan(
        one_block,
        start_sum,
        (
            split_rows(queries),
            split_rows(keys_all),
            split_rows(values_all),
            split_rows(grads),
            split_rows(mask_all),
        ),
    )
    return (
        stacked[0].reshape(row_count, query_count, channel_count),
        stacked[1].reshape(row_count, key_count, channel_count),
        stacked[2].reshape(row_count, key_count, channel_count),
        bias_sum,
    )


def local(query_proj, key_proj, value_proj, pair_bias, pair_mask, grad_out):
    bias_rows = lax.all_gather(pair_bias, "row", axis=2, tiled=True)
    mask_low = pair_mask.astype(jnp.bfloat16)
    local_tiles = (
        lax.all_to_all(query_proj, "col", split_axis=0, concat_axis=1, tiled=True),
        lax.all_to_all(key_proj, "col", split_axis=0, concat_axis=1, tiled=True),
        lax.all_to_all(value_proj, "col", split_axis=0, concat_axis=1, tiled=True),
        lax.all_to_all(grad_out, "col", split_axis=0, concat_axis=1, tiled=True),
        lax.all_to_all(mask_low, "col", split_axis=0, concat_axis=1, tiled=True),
    )
    bias_full = lax.all_gather(bias_rows, "col", axis=1, tiled=True)
    grad_queries, grad_keys, grad_values, bias_whole = all_blocks(
        local_tiles[0], local_tiles[1], local_tiles[2], local_tiles[3], local_tiles[4], bias_full
    )
    grad_query, grad_key, grad_value = (
        lax.all_to_all(
            grad_queries.astype(jnp.bfloat16), "col", split_axis=1, concat_axis=0, tiled=True
        ),
        lax.all_to_all(
            grad_keys.astype(jnp.bfloat16), "col", split_axis=1, concat_axis=0, tiled=True
        ),
        lax.all_to_all(
            grad_values.astype(jnp.bfloat16), "col", split_axis=1, concat_axis=0, tiled=True
        ),
    )
    bias_part = lax.psum_scatter(bias_whole, "col", scatter_dimension=1, tiled=True)
    grad_bias = lax.psum_scatter(bias_part, "row", scatter_dimension=2, tiled=True)
    return (grad_query, grad_key, grad_value, grad_bias)


def solution(mesh):
    placed = (
        P("row", "col", None),
        P("row", "col", None),
        P("row", "col", None),
        P(None, "col", "row"),
        P("row", "col"),
        P("row", "col", None),
    )
    return jax.shard_map(
        local,
        mesh=mesh,
        in_specs=placed,
        out_specs=(
            P("row", "col", None),
            P("row", "col", None),
            P("row", "col", None),
            P(None, "col", "row"),
        ),
        check_vma=False,
    )
```

profile of v0, /device:TPU:0, one launch (start us, length us, event | category | flops | bytes accessed | tf_op | source)
XLA Modules:
  0.0 196.8 jit_solution(4565069296105848895)
XLA Ops:
  7.2 0.7 convert_element_type.60
  8.0 11.7 %all_to_all.130 = bf16[4,2,144]{2,1,0:T(2,128)(2,1)S(1)} all-to-all(bf16[4,2,144]{2,1,0:T(2,128)(2,1)S(1)} %reshape.104), channel_id=1, replica_groups=mesh['row'=8,'col'=4] {'col'}, dimensions={0} | all-to-all | bytes 4608 | tf_op jit(solution)/shard_map/all_to_all | solution.py:108
  19.7 11.8 %all_to_all.131 = bf16[24,48,128]{2,1,0:T(8,128)(2,1)S(1)} all-to-all(bf16[24,48,128]{2,1,0:T(8,128)(2,1)} %param.8), channel_id=1, replica_groups=mesh['row'=8,'col'=4] {'col'}, dimensions={0} | all-to-all | bytes 589824 | tf_op jit(solution)/shard_map/all_to_all | solution.py:104
  31.6 11.7 %all_to_all.132 = bf16[24,48,128]{2,1,0:T(8,128)(2,1)S(1)} all-to-all(bf16[24,48,128]{2,1,0:T(8,128)(2,1)} %param.9), channel_id=1, replica_groups=mesh['row'=8,'col'=4] {'col'}, dimensions={0} | all-to-all | bytes 589824 | tf_op jit(solution)/shard_map/all_to_all | solution.py:105
  43.3 11.6 %all_to_all.133 = bf16[24,48,128]{2,1,0:T(8,128)(2,1)S(1)} all-to-all(bf16[24,48,128]{2,1,0:T(8,128)(2,1)} %param.10), channel_id=1, replica_groups=mesh['row'=8,'col'=4] {'col'}, dimensions={0} | all-to-all | bytes 589824 | tf_op jit(solution)/shard_map/all_to_all | solution.py:106
  54.9 3.5 %all-to-all-start.3 = ((bf16[24,48,128]{2,1,0:T(8,128)(2,1)}), bf16[24,48,128]{2,1,0:T(8,128)(2,1)S(1)}, u32[]{:S(2)}, u32[]{:S(2)}) async-start(bf16[24,48,128]{2,1,0:T(8,128)(2,1)} %param.13), calls=%async_computation.3 | async-start | bytes 589824 | tf_op jit(solution)/shard_map/all_to_all | solution.py:107
  58.5 9.3 %all_gather.6 = bf16[4,48,192]{1,0,2:T(4,128)(2,1)S(1)} all-gather(bf16[4,48,24]{1,0,2:T(4,128)(2,1)S(1)} %copy.115), channel_id=1, replica_groups=mesh['row'=8,'col'=4] {'row'}, dimensions={2}, use_global_device_ids=true | all-gather | bytes 82944 | tf_op jit(solution)/shard_map/all_gather | solution.py:101
  67.9 15.1 %all_gather.7 = bf16[4,192,192]{2,0,1:T(4,128)(2,1)S(1)} all-gather(bf16[4,48,192]{2,0,1:T(4,128)(2,1)S(1)} %copy.116), channel_id=1, replica_groups=mesh['row'=8,'col'=4] {'col'}, dimensions={1}, use_global_device_ids=true | all-gather | bytes 368640 | tf_op jit(solution)/shard_map/all_gather | solution.py:110
  83.1 0.3 copy.122
  83.6 0.7 copy.113
  84.4 23.5 %while.19 = (s32[]{:T(128)}, f32[4,192,192]{1,2,0:T(8,128)S(1)}, bf16[3,2,192,128]{3,2,1,0:T(8,128)(2,1)}, bf16[3,2,192,128]{3,2,1,0:T(8,128)(2,1)}, bf16[3,2,19...) while((s32[]{:T(128)}, f32[4,192,192]{1,2,0:T(8,128)S(1)}, ...), condition=%wide.region_5.6_spmd.clone, body=%wide.region_0.5_spmd.clone.sunk | while | flops 117423936 | bytes 24709288 | solution.py:81
  84.5 0.9 copy.164
  85.7 0.9 constant_dynamic-slice_fusion.10
  86.8 0.8 fusion.54
  87.8 0.7 copy-done.2
  88.5 0.3 fusion.56
  88.8 0.3 fusion.58
  89.2 0.5 fusion.57
  89.7 0.2 select_add_fusion.2
  90.0 0.3 convolution_multiply_fusion.5
  90.4 0.3 convolution_multiply_fusion.4
  90.9 0.7 constant_dynamic-update-slice_fusion.5
  91.5 0.7 constant_dynamic-update-slice_fusion.6
  92.3 0.9 copy.164
  93.5 0.9 constant_dynamic-slice_fusion.10
  94.7 0.8 fusion.54
  95.6 0.7 copy-done.2
  96.3 0.3 fusion.56
  96.6 0.3 fusion.58
  97.1 0.5 fusion.57
  97.6 0.2 select_add_fusion.2
  97.9 0.3 convolution_multiply_fusion.5
  98.2 0.3 convolution_multiply_fusion.4
  98.7 0.7 constant_dynamic-update-slice_fusion.5
  99.4 0.7 constant_dynamic-update-slice_fusion.6
  100.2 0.9 copy.164
  101.4 0.9 constant_dynamic-slice_fusion.10
  102.5 0.8 fusion.54
  103.4 0.7 copy-done.2
  104.2 0.3 fusion.56
  104.5 0.3 fusion.58
  104.9 0.5 fusion.57
  105.4 0.2 select_add_fusion.2
  105.7 0.3 convolution_multiply_fusion.5
  106.0 0.3 convolution_multiply_fusion.4
  106.5 0.7 constant_dynamic-update-slice_fusion.5
  107.2 0.7 constant_dynamic-update-slice_fusion.6
  107.9 0.4 copy.145
  108.3 1.3 reshape.102
  109.6 1.9 copy.134
  111.5 5.4 %all-to-all-start.7 = ((bf16[6,192,128]{2,0,1:T(8,128)(2,1)}), bf16[6,192,128]{2,0,1:T(8,128)(2,1)S(1)}, u32[]{:S(2)}, u32[]{:S(2)}) async-start(bf16[6,192,128]{2,0,1:T(8,128)(2,1)} %copy.134), calls=%async_computation.7 | async-start | bytes 786432 | tf_op jit(solution)/shard_map/all_to_all | solution.py:121
  116.9 1.0 copy.126
  117.9 17.4 %all-to-all-done.7 = bf16[6,192,128]{2,0,1:T(8,128)(2,1)S(1)} async-done(((bf16[6,192,128]{2,0,1:T(8,128)(2,1)}), bf16[6,192,128]{2,0,1:T(8,128)(2,1)S(1)}, u32[]{:S(2)}, u32[]{:S(2)}) %all-to-all-start.7) | async-done | bytes 294944 | tf_op jit(solution)/shard_map/all_to_all | solution.py:121
  135.3 3.5 %all-to-all-start.5 = ((bf16[6,192,128]{2,0,1:T(8,128)(2,1)}), bf16[6,192,128]{2,0,1:T(8,128)(2,1)S(1)}, u32[]{:S(2)}, u32[]{:S(2)}) async-start(bf16[6,192,128]{2,0,1:T(8,128)(2,1)} %copy.126), calls=%async_computation.5 | async-start | bytes 786432 | tf_op jit(solution)/shard_map/all_to_all | solution.py:115
  138.8 1.9 copy.130
  140.7 6.9 %all-to-all-done.5 = bf16[6,192,128]{2,0,1:T(8,128)(2,1)S(1)} async-done(((bf16[6,192,128]{2,0,1:T(8,128)(2,1)}), bf16[6,192,128]{2,0,1:T(8,128)(2,1)S(1)}, u32[]{:S(2)}, u32[]{:S(2)}) %all-to-all-start.5) | async-done | bytes 294944 | tf_op jit(solution)/shard_map/all_to_all | solution.py:115
  147.6 3.5 %all-to-all-start.6 = ((bf16[6,192,128]{2,0,1:T(8,128)(2,1)}), bf16[6,192,128]{2,0,1:T(8,128)(2,1)S(1)}, u32[]{:S(2)}, u32[]{:S(2)}) async-start(bf16[6,192,128]{2,0,1:T(8,128)(2,1)} %copy.130), calls=%async_computation.6 | async-start | bytes 786432 | tf_op jit(solution)/shard_map/all_to_all | solution.py:118
  151.2 1.1 reshape.103
  152.2 0.9 copy.146
  153.2 0.8 copy.136
  154.0 0.8 copy.128
  154.7 5.2 %all-to-all-done.6 = bf16[6,192,128]{2,0,1:T(8,128)(2,1)S(1)} async-done(((bf16[6,192,128]{2,0,1:T(8,128)(2,1)}), bf16[6,192,128]{2,0,1:T(8,128)(2,1)S(1)}, u32[]{:S(2)}, u32[]{:S(2)}) %all-to-all-start.6) | async-done | bytes 294944 | tf_op jit(solution)/shard_map/all_to_all | solution.py:118
  160.0 0.8 copy.132
  160.7 29.2 %reduce-scatter.5.cloned.1.call-done = f32[4,48,24]{1,2,0:T(8,128)} async-done(((f32[4,48,192]{1,2,0:T(8,128)}), f32[4,48,24]{1,2,0:T(8,128)}) %reduce-scatter.5.cloned.1.call-update) | async-done | bytes 18448 | tf_op jit(solution)/shard_map/reduce_scatter | solution.py:126
  (111 shorter events, 3.7 us)
Async XLA Ops:
  7.2 51.3 %copy-start.10 = (bf16[4,48,24]{1,2,0:T(8,128)(2,1)S(1)}, bf16[4,48,24]{1,2,0:T(8,128)(2,1)}, u32[]{:S(2)}) copy-start(bf16[4,48,24]{1,2,0:T(8,128)(2,1)} %param.11) | copy-start | bytes 27652
  54.9 29.4 %all-to-all-start.3 = ((bf16[24,48,128]{2,1,0:T(8,128)(2,1)}), bf16[24,48,128]{2,1,0:T(8,128)(2,1)S(1)}, u32[]{:S(2)}, u32[]{:S(2)}) async-start(bf16[24,48,128]{2,1,0:T(8,128)(2,1)} %param.13), calls=%async_computation.3 | async-start | bytes 589824 | tf_op jit(solution)/shard_map/all_to_all | solution.py:107
  58.4 92.8 %reduce-scatter.7.cloned.1.call-start = ((), (), s32[]{:S(2)}) async-start(), calls=%async_computation.11 | async-start | bytes 737280
  84.4 2.3 %copy-start = (bf16[4,192,192]{1,2,0:T(8,128)(2,1)}, bf16[4,192,192]{1,2,0:T(8,128)(2,1)S(1)}, u32[]{:S(2)}) copy-start(bf16[4,192,192]{1,2,0:T(8,128)(2,1)S(1)} %get-tuple-element.381) | copy-start | bytes 884740 | tf_op jit(solution)/shard_map/while
  84.4 2.3 %copy-start.3 = (bf16[3,2,192,128]{3,2,1,0:T(8,128)(2,1)}, bf16[3,2,192,128]{3,2,1,0:T(8,128)(2,1)S(1)}, u32[]{:S(2)}) copy-start(bf16[3,2,192,128]{3,2,1,0:T(8,128)(2,1)S(1)} %get-tuple-element.380) | copy-start | bytes 884740 | tf_op jit(solution)/shard_map/while
  84.4 2.3 %copy-start.5 = (bf16[3,2,192,128]{3,2,1,0:T(8,128)(2,1)}, bf16[3,2,192,128]{3,2,1,0:T(8,128)(2,1)S(1)}, u32[]{:S(2)}) copy-start(bf16[3,2,192,128]{3,2,1,0:T(8,128)(2,1)S(1)} %get-tuple-element.384) | copy-start | bytes 884740 | tf_op jit(solution)/shard_map/while
  84.4 2.3 %copy-start.7 = (bf16[3,2,192,128]{3,2,1,0:T(8,128)(2,1)}, bf16[3,2,192,128]{3,2,1,0:T(8,128)(2,1)S(1)}, u32[]{:S(2)}) copy-start(bf16[3,2,192,128]{3,2,1,0:T(8,128)(2,1)S(1)} %get-tuple-element.383) | copy-start | bytes 884740 | tf_op jit(solution)/shard_map/while
  87.6 0.9 copy-start.2
  90.0 2.2 %copy-start.1 = (bf16[4,192,192]{1,2,0:T(8,128)(2,1)S(1)}, bf16[4,192,192]{1,2,0:T(8,128)(2,1)}, u32[]{:S(2)}) copy-start(bf16[4,192,192]{1,2,0:T(8,128)(2,1)} %copy-done) | copy-start | bytes 884740 | tf_op jit(solution)/shard_map/while
  90.0 2.2 %copy-start.4 = (bf16[3,2,192,128]{3,2,1,0:T(8,128)(2,1)S(1)}, bf16[3,2,192,128]{3,2,1,0:T(8,128)(2,1)}, u32[]{:S(2)}) copy-start(bf16[3,2,192,128]{3,2,1,0:T(8,128)(2,1)} %copy-done.3) | copy-start | bytes 884740 | tf_op jit(solution)/shard_map/while
  90.0 2.2 %copy-start.6 = (bf16[3,2,192,128]{3,2,1,0:T(8,128)(2,1)S(1)}, bf16[3,2,192,128]{3,2,1,0:T(8,128)(2,1)}, u32[]{:S(2)}) copy-start(bf16[3,2,192,128]{3,2,1,0:T(8,128)(2,1)} %copy-done.5) | copy-start | bytes 884740 | tf_op jit(solution)/shard_map/while
  90.0 2.2 %copy-start.8 = (bf16[3,2,192,128]{3,2,1,0:T(8,128)(2,1)S(1)}, bf16[3,2,192,128]{3,2,1,0:T(8,128)(2,1)}, u32[]{:S(2)}) copy-start(bf16[3,2,192,128]{3,2,1,0:T(8,128)(2,1)} %copy-done.7) | copy-start | bytes 884740 | tf_op jit(solution)/shard_map/while
  92.2 2.3 %copy-start = (bf16[4,192,192]{1,2,0:T(8,128)(2,1)}, bf16[4,192,192]{1,2,0:T(8,128)(2,1)S(1)}, u32[]{:S(2)}) copy-start(bf16[4,192,192]{1,2,0:T(8,128)(2,1)S(1)} %get-tuple-element.381) | copy-start | bytes 884740 | tf_op jit(solution)/shard_map/while
  92.3 2.3 %copy-start.3 = (bf16[3,2,192,128]{3,2,1,0:T(8,128)(2,1)}, bf16[3,2,192,128]{3,2,1,0:T(8,128)(2,1)S(1)}, u32[]{:S(2)}) copy-start(bf16[3,2,192,128]{3,2,1,0:T(8,128)(2,1)S(1)} %get-tuple-element.380) | copy-start | bytes 884740 | tf_op jit(solution)/shard_map/while
  92.3 2.3 %copy-start.5 = (bf16[3,2,192,128]{3,2,1,0:T(8,128)(2,1)}, bf16[3,2,192,128]{3,2,1,0:T(8,128)(2,1)S(1)}, u32[]{:S(2)}) copy-start(bf16[3,2,192,128]{3,2,1,0:T(8,128)(2,1)S(1)} %get-tuple-element.384) | copy-start | bytes 884740 | tf_op jit(solution)/shard_map/while
  92.3 2.3 %copy-start.7 = (bf16[3,2,192,128]{3,2,1,0:T(8,128)(2,1)}, bf16[3,2,192,128]{3,2,1,0:T(8,128)(2,1)S(1)}, u32[]{:S(2)}) copy-start(bf16[3,2,192,128]{3,2,1,0:T(8,128)(2,1)S(1)} %get-tuple-element.383) | copy-start | bytes 884740 | tf_op jit(solution)/shard_map/while
  95.4 0.9 copy-start.2
  97.8 2.2 %copy-start.1 = (bf16[4,192,192]{1,2,0:T(8,128)(2,1)S(1)}, bf16[4,192,192]{1,2,0:T(8,128)(2,1)}, u32[]{:S(2)}) copy-start(bf16[4,192,192]{1,2,0:T(8,128)(2,1)} %copy-done) | copy-start | bytes 884740 | tf_op jit(solution)/shard_map/while
  97.8 2.2 %copy-start.4 = (bf16[3,2,192,128]{3,2,1,0:T(8,128)(2,1)S(1)}, bf16[3,2,192,128]{3,2,1,0:T(8,128)(2,1)}, u32[]{:S(2)}) copy-start(bf16[3,2,192,128]{3,2,1,0:T(8,128)(2,1)} %copy-done.3) | copy-start | bytes 884740 | tf_op jit(solution)/shard_map/while
  97.8 2.2 %copy-start.6 = (bf16[3,2,192,128]{3,2,1,0:T(8,128)(2,1)S(1)}, bf16[3,2,192,128]{3,2,1,0:T(8,128)(2,1)}, u32[]{:S(2)}) copy-start(bf16[3,2,192,128]{3,2,1,0:T(8,128)(2,1)} %copy-done.5) | copy-start | bytes 884740 | tf_op jit(solution)/shard_map/while
  97.8 2.2 %copy-start.8 = (bf16[3,2,192,128]{3,2,1,0:T(8,128)(2,1)S(1)}, bf16[3,2,192,128]{3,2,1,0:T(8,128)(2,1)}, u32[]{:S(2)}) copy-start(bf16[3,2,192,128]{3,2,1,0:T(8,128)(2,1)} %copy-done.7) | copy-start | bytes 884740 | tf_op jit(solution)/shard_map/while
  100.1 2.3 %copy-start = (bf16[4,192,192]{1,2,0:T(8,128)(2,1)}, bf16[4,192,192]{1,2,0:T(8,128)(2,1)S(1)}, u32[]{:S(2)}) copy-start(bf16[4,192,192]{1,2,0:T(8,128)(2,1)S(1)} %get-tuple-element.381) | copy-start | bytes 884740 | tf_op jit(solution)/shard_map/while
  100.1 2.3 %copy-start.3 = (bf16[3,2,192,128]{3,2,1,0:T(8,128)(2,1)}, bf16[3,2,192,128]{3,2,1,0:T(8,128)(2,1)S(1)}, u32[]{:S(2)}) copy-start(bf16[3,2,192,128]{3,2,1,0:T(8,128)(2,1)S(1)} %get-tuple-element.380) | copy-start | bytes 884740 | tf_op jit(solution)/shard_map/while
  100.1 2.3 %copy-start.5 = (bf16[3,2,192,128]{3,2,1,0:T(8,128)(2,1)}, bf16[3,2,192,128]{3,2,1,0:T(8,128)(2,1)S(1)}, u32[]{:S(2)}) copy-start(bf16[3,2,192,128]{3,2,1,0:T(8,128)(2,1)S(1)} %get-tuple-element.384) | copy-start | bytes 884740 | tf_op jit(solution)/shard_map/while
  100.1 2.3 %copy-start.7 = (bf16[3,2,192,128]{3,2,1,0:T(8,128)(2,1)}, bf16[3,2,192,128]{3,2,1,0:T(8,128)(2,1)S(1)}, u32[]{:S(2)}) copy-start(bf16[3,2,192,128]{3,2,1,0:T(8,128)(2,1)S(1)} %get-tuple-element.383) | copy-start | bytes 884740 | tf_op jit(solution)/shard_map/while
  103.3 0.9 copy-start.2
  105.6 2.2 %copy-start.1 = (bf16[4,192,192]{1,2,0:T(8,128)(2,1)S(1)}, bf16[4,192,192]{1,2,0:T(8,128)(2,1)}, u32[]{:S(2)}) copy-start(bf16[4,192,192]{1,2,0:T(8,128)(2,1)} %copy-done) | copy-start | bytes 884740 | tf_op jit(solution)/shard_map/while
  105.7 2.2 %copy-start.4 = (bf16[3,2,192,128]{3,2,1,0:T(8,128)(2,1)S(1)}, bf16[3,2,192,128]{3,2,1,0:T(8,128)(2,1)}, u32[]{:S(2)}) copy-start(bf16[3,2,192,128]{3,2,1,0:T(8,128)(2,1)} %copy-done.3) | copy-start | bytes 884740 | tf_op jit(solution)/shard_map/while
  105.7 2.2 %copy-start.6 = (bf16[3,2,192,128]{3,2,1,0:T(8,128)(2,1)S(1)}, bf16[3,2,192,128]{3,2,1,0:T(8,128)(2,1)}, u32[]{:S(2)}) copy-start(bf16[3,2,192,128]{3,2,1,0:T(8,128)(2,1)} %copy-done.5) | copy-start | bytes 884740 | tf_op jit(solution)/shard_map/while
  105.7 2.2 %copy-start.8 = (bf16[3,2,192,128]{3,2,1,0:T(8,128)(2,1)S(1)}, bf16[3,2,192,128]{3,2,1,0:T(8,128)(2,1)}, u32[]{:S(2)}) copy-start(bf16[3,2,192,128]{3,2,1,0:T(8,128)(2,1)} %copy-done.7) | copy-start | bytes 884740 | tf_op jit(solution)/shard_map/while
  108.3 8.6 %copy-start.9 = (bf16[3,2,192,128]{3,2,1,0:T(8,128)(2,1)S(1)}, bf16[3,2,192,128]{3,2,1,0:T(8,128)(2,1)}, u32[]{:S(2)}) copy-start(bf16[3,2,192,128]{3,2,1,0:T(8,128)(2,1)} %get-tuple-element.144) | copy-start | bytes 884740
  111.5 23.8 %all-to-all-start.7 = ((bf16[6,192,128]{2,0,1:T(8,128)(2,1)}), bf16[6,192,128]{2,0,1:T(8,128)(2,1)S(1)}, u32[]{:S(2)}, u32[]{:S(2)}) async-start(bf16[6,192,128]{2,0,1:T(8,128)(2,1)} %copy.134), calls=%async_computation.7 | async-start | bytes 786432 | tf_op jit(solution)/shard_map/all_to_all | solution.py:121
  135.3 12.3 %all-to-all-start.5 = ((bf16[6,192,128]{2,0,1:T(8,128)(2,1)}), bf16[6,192,128]{2,0,1:T(8,128)(2,1)S(1)}, u32[]{:S(2)}, u32[]{:S(2)}) async-start(bf16[6,192,128]{2,0,1:T(8,128)(2,1)} %copy.126), calls=%async_computation.5 | async-start | bytes 786432 | tf_op jit(solution)/shard_map/all_to_all | solution.py:115
  147.6 12.3 %all-to-all-start.6 = ((bf16[6,192,128]{2,0,1:T(8,128)(2,1)}), bf16[6,192,128]{2,0,1:T(8,128)(2,1)S(1)}, u32[]{:S(2)}, u32[]{:S(2)}) async-start(bf16[6,192,128]{2,0,1:T(8,128)(2,1)} %copy.130), calls=%async_computation.6 | async-start | bytes 786432 | tf_op jit(solution)/shard_map/all_to_all | solution.py:118
  151.1 38.8 %reduce-scatter.5.cloned.1.call-start = ((), (), s32[]{:S(2)}) async-start(), calls=%async_computation.10 | async-start | bytes 442368 | tf_op jit(solution)/shard_map/reduce_scatter | solution.py:126
Sparse Core Ops, SparseCore 0:
  109.7 25.3 reduce-scatter.6
  155.6 34.3 reduce-scatter.4
where the time goes:
time: 198 us; the launch traced here: 197 us
  blocking collectives  71.3 us (36%)
  waiting for transfers between devices  58.9 us (30%)
  local copies, waits for them, and re-layouts  26.4 us (13%)
  starting transfers between devices  15.8 us (8%)
  between operations  14.2 us (7%)
  matrix products  7.33 us (4%)
  other arithmetic  2.1 us (1%)
    reduce_scatter x1, waiting for transfers between devices, local(): lax.psum_scatter(bias_part, 'row', scatter_dimension=2, tiled=True)  29.2 us
    all_to_all x1, waiting for transfers between devices, local(): lax.all_to_all(grad_values.astype(jnp.bfloat16), 'col', split_axis=1, con...  17.4 us
    all_gather x1, blocking collectives, local(): bias_full = lax.all_gather(bias_rows, 'col', axis=1, tiled=True)  15.1 us
    all_to_all x1, blocking collectives, local(): lax.all_to_all(query_proj, 'col', split_axis=0, concat_axis=1, tiled=True)  11.8 us
    all_to_all x1, blocking collectives, local(): lax.all_to_all(key_proj, 'col', split_axis=0, concat_axis=1, tiled=True)  11.7 us
    all_to_all x1, blocking collectives, local(): lax.all_to_all(mask_low, 'col', split_axis=0, concat_axis=1, tiled=True)  11.7 us
    all_to_all x1, blocking collectives, local(): lax.all_to_all(value_proj, 'col', split_axis=0, concat_axis=1, tiled=True)  11.6 us
    all_gather x1, blocking collectives, local(): bias_rows = lax.all_gather(pair_bias, 'row', axis=2, tiled=True)  9.27 us
  transfers between devices with their start and end apart: 6, of which 4 were waited for; matrix products, arithmetic and copies ran while one was open for 5% of the time, Pallas kernels for 0%

commit v1 on v0

--- a/solution.py
+++ b/solution.py
@@ -1,8 +1,11 @@
+import functools
 import math
 
 import jax
 import jax.numpy as jnp
 from jax import lax
+from jax.experimental import pallas as pl
+from jax.experimental.pallas import tpu as pltpu
 from jax.sharding import PartitionSpec as P
 
 HEADS = 4
@@ -127,6 +130,324 @@
     return (grad_query, grad_key, grad_value, grad_bias)
 
 
+MESH = pl.DeviceIdType.MESH
+
+
+def round_up(value, step):
+    return -(-value // step) * step
+
+
+def fused_kernel(
+    rows_n, cols_n, pack,
+    q_ref, k_ref, v_ref, g_ref, bias_ref, mask_ref,
+    gq_ref, gk_ref, gv_ref, gb_ref,
+    got, stage, bias_all, mask_all, bias_full, bias_sum, part, part_in, tile, tile_in,
+    in_send, in_recv, out_send, out_recv, bc_send, bc_recv, br_send, br_recv,
+    mk_send, mk_recv, pr_send, pr_recv, pc_send, pc_recv, own_sem,
+):
+    row, col = lax.axis_index("row"), lax.axis_index("col")
+    per = got.shape[1]
+    count = got.shape[2]
+    width = q_ref.shape[1]
+    keys = bias_sum.shape[1] // rows_n
+    packs, padded, lanes = bias_ref.shape
+    chunk = 2 if per % 2 == 0 else 1
+    chunks = per // chunk
+    scale = 1.0 / math.sqrt(HEAD_DIM)
+    sources = (q_ref, k_ref, v_ref, g_ref)
+    results = (gq_ref, gk_ref, gv_ref)
+
+    def row_peer(d):
+        return (lax.rem(row + d, rows_n), col)
+
+    def col_peer(d):
+        return (row, lax.rem(col + d, cols_n))
+
+    def remote(src, dst, send, recv, peer):
+        return pltpu.make_async_remote_copy(
+            src_ref=src, dst_ref=dst, send_sem=send, recv_sem=recv,
+            device_id=peer, device_id_type=MESH,
+        )
+
+    barrier = pltpu.get_barrier_semaphore()
+    for d in range(1, rows_n):
+        pl.semaphore_signal(barrier, inc=1, device_id=row_peer(d), device_id_type=MESH)
+    for d in range(1, cols_n):
+        pl.semaphore_signal(barrier, inc=1, device_id=col_peer(d), device_id_type=MESH)
+    pl.semaphore_wait(barrier, rows_n + cols_n - 2)
+
+    my_cols = pl.ds(pl.multiple_of(col * width, width), width)
+    bias_col = [
+        remote(bias_ref, bias_all.at[row, col], bc_send.at[d], bc_recv.at[d], col_peer(d))
+        for d in range(1, cols_n)
+    ]
+    mask_col = [
+        remote(mask_ref, mask_all.at[my_cols], mk_send.at[d], mk_recv.at[d], col_peer(d))
+        for d in range(1, cols_n)
+    ]
+    for copy in bias_col + mask_col:
+        copy.start()
+    own = [
+        pltpu.make_async_copy(bias_ref, bias_all.at[row, col], own_sem.at[0]),
+        pltpu.make_async_copy(mask_ref, mask_all.at[my_cols], own_sem.at[1]),
+    ]
+    for a in range(4):
+        own.append(pltpu.make_async_copy(
+            sources[a].at[pl.ds(col * per, per)], got.at[a, :, my_cols], own_sem.at[2 + a]
+        ))
+    for copy in own:
+        copy.start()
+
+    def in_copies(c):
+        copies = []
+        for d in range(1, cols_n):
+            peer = col_peer(d)
+            for a in range(4):
+                copies.append(remote(
+                    sources[a].at[pl.ds(peer[1] * per + c * chunk, chunk)],
+                    got.at[a, pl.ds(c * chunk, chunk), my_cols],
+                    in_send.at[c, d, a], in_recv.at[c, d, a], peer,
+                ))
+        return copies
+
+    def out_copies(c):
+        copies = []
+        for d in range(1, cols_n):
+            peer = col_peer(d)
+            there = pl.ds(pl.multiple_of(peer[1] * width, width), width)
+            for a in range(3):
+                copies.append(remote(
+                    stage.at[a, pl.ds(c * chunk, chunk), there],
+                    results[a].at[pl.ds(col * per + c * chunk, chunk)],
+                    out_send.at[c, d, a], out_recv.at[c, d, a], peer,
+                ))
+        return copies
+
+    def own_outs(c):
+        return [
+            pltpu.make_async_copy(
+                stage.at[a, pl.ds(c * chunk, chunk), my_cols],
+                results[a].at[pl.ds(col * per + c * chunk, chunk)],
+                out_send.at[c, 0, a],
+            )
+            for a in range(3)
+        ]
+
+    @pl.loop(0, chunks)
+    def _(c):
+        for copy in in_copies(c):
+            copy.start()
+
+    for copy in bias_col:
+        copy.wait_recv()
+    for copy in own:
+        copy.wait()
+    bias_row = [
+        remote(bias_all.at[row], bias_all.at[row], br_send.at[d], br_recv.at[d], row_peer(d))
+        for d in range(1, rows_n)
+    ]
+    for copy in bias_row:
+        copy.start()
+    bias_sum[...] = jnp.zeros_like(bias_sum)
+    part[...] = jnp.zeros_like(part)
+    for copy in mask_col:
+        copy.wait_recv()
+    for copy in bias_row:
+        copy.wait_recv()
+
+    def pick(z, hh, shape, lane_axis):
+        lane = lax.broadcasted_iota(jnp.int32, shape, lane_axis)
+        at = lax.broadcasted_iota(jnp.int32, shape, 1 - lane_axis)
+        inside = (lane >= hh * width) & (lane < (hh + 1) * width)
+        return jnp.where(inside & (lane + (z - hh) * width == at), 1.0, 0.0).astype(jnp.bfloat16)
+
+    for p in range(packs):
+        for hh in range(pack):
+            whole = jnp.zeros((rows_n * padded, count), jnp.float32)
+            for z in range(cols_n):
+                piece = bias_all[:, z, p].reshape(rows_n * padded, lanes)
+                whole = whole + jnp.dot(
+                    piece, pick(z, hh, (lanes, count), 0), preferred_element_type=jnp.float32
+                )
+            for r in range(rows_n):
+                bias_full[p * pack + hh, r * keys:(r + 1) * keys, :] = (
+                    whole[r * padded:r * padded + keys]
+                )
+
+    nt = (((1,), (1,)), ((), ()))
+    tn = (((0,), (0,)), ((), ()))
+    channel = lax.broadcasted_iota(jnp.int32, (count, HEADS * HEAD_DIM), 1)
+    mask_lane = lax.broadcasted_iota(jnp.int32, mask_all.shape, 1)
+
+    def one_row(i):
+        q, k, v, g = got[0, i], got[1, i], got[2, i], got[3, i]
+        present = jnp.sum(
+            jnp.where(mask_lane == col * per + i, mask_all[...].astype(jnp.float32), 0.0),
+            axis=1, keepdims=True,
+        )
+        masked = 1000000000.0 * (present - 1.0)
+        gq = jnp.zeros((count, HEADS * HEAD_DIM), jnp.float32)
+        gk = gq
+        gv = gq
+        for h in range(HEADS):
+            mine = (channel >= h * HEAD_DIM) & (channel < (h + 1) * HEAD_DIM)
+
+            def only(x):
+                return jnp.where(mine, x, jnp.zeros_like(x))
+
+            kh, vh, qh, gh = only(k), only(v), only(q), only(g)
+            scores = lax.dot_general(kh, q, nt, preferred_element_type=jnp.float32) * scale
+            scores = scores + bias_full[h] + masked
+            weights = jnp.exp(scores - jnp.max(scores, axis=0, keepdims=True))
+            probs = weights * (1.0 / jnp.sum(weights, axis=0, keepdims=True))
+            low = probs.astype(jnp.bfloat16)
+            grad_probs = lax.dot_general(vh, g, nt, preferred_element_type=jnp.float32)
+            delta = jnp.sum(low.astype(jnp.float32) * grad_probs, axis=0, keepdims=True)
+            grad_scores = probs * (grad_probs - delta)
+            bias_sum[h] += grad_scores
+            slow = grad_scores.astype(jnp.bfloat16)
+            gq = gq + lax.dot_general(slow, kh, tn, preferred_element_type=jnp.float32)
+            gk = gk + jnp.dot(slow, qh, preferred_element_type=jnp.float32)
+            gv = gv + jnp.dot(low, gh, preferred_element_type=jnp.float32)
+        stage[0, i] = (gq * scale).astype(jnp.bfloat16)
+        stage[1, i] = (gk * scale).astype(jnp.bfloat16)
+        stage[2, i] = gv.astype(jnp.bfloat16)
+
+    @pl.loop(0, chunks)
+    def _(c):
+        for copy in in_copies(c):
+            copy.wait_recv()
+
+        @pl.loop(0, chunk)
+        def _(r):
+            one_row(c * chunk + r)
+
+        for copy in out_copies(c) + own_outs(c):
+            copy.start()
+
+    for r in range(rows_n):
+        for h in range(HEADS):
+            part[r, h, 0:keys, :] = bias_sum[h, r * keys:(r + 1) * keys, :].astype(jnp.bfloat16)
+    part_row = []
+    for d in range(1, rows_n):
+        peer = row_peer(d)
+        part_row.append(remote(
+            part.at[peer[0]], part_in.at[row], pr_send.at[d], pr_recv.at[d], peer
+        ))
+    for copy in part_row:
+        copy.start()
+    for copy in part_row:
+        copy.wait_recv()
+    sums = []
+    for h in range(HEADS):
+        total = part[row, h].astype(jnp.float32)
+        for d in range(1, rows_n):
+            total = total + part_in[lax.rem(row + d, rows_n), h].astype(jnp.float32)
+        sums.append(total.astype(jnp.bfloat16))
+    for z in range(cols_n):
+        for p in range(packs):
+            packed = jnp.zeros((padded, lanes), jnp.float32)
+            for hh in range(pack):
+                packed = packed + jnp.dot(
+                    sums[p * pack + hh], pick(z, hh, (count, lanes), 1),
+                    preferred_element_type=jnp.float32,
+                )
+            tile[z, p] = packed.astype(jnp.bfloat16)
+    part_col = []
+    for d in range(1, cols_n):
+        peer = col_peer(d)
+        part_col.append(remote(
+            tile.at[peer[1]], tile_in.at[col], pc_send.at[d], pc_recv.at[d], peer
+        ))
+    for copy in part_col:
+        copy.start()
+    for copy in part_col:
+        copy.wait_recv()
+    total = tile[col].astype(jnp.float32)
+    for d in range(1, cols_n):
+        total = total + tile_in[lax.rem(col + d, cols_n)].astype(jnp.float32)
+    gb_ref[...] = total
+
+    @pl.loop(0, chunks)
+    def _(c):
+        for copy in in_copies(c):
+            copy.wait_send()
+        for copy in out_copies(c):
+            copy.wait()
+        for copy in own_outs(c):
+            copy.wait()
+
+    for copy in bias_col + mask_col + bias_row + part_row + part_col:
+        copy.wait_send()
+
+
+def fused(rows_n, cols_n, query_proj, key_proj, value_proj, pair_bias, pair_mask, grad_out):
+    rows, width, channels = query_proj.shape
+    keys = pair_bias.shape[2]
+    per, count = rows // cols_n, width * cols_n
+    pack = 1
+    while pack * 2 <= HEADS and pack * 2 * width <= 128:
+        pack = pack * 2
+    packs = HEADS // pack
+    padded, lanes = round_up(keys, 16), round_up(pack * width, 128)
+    flipped = jnp.transpose(pair_bias, (0, 2, 1)).reshape(packs, pack, keys, width)
+    flipped = jnp.transpose(flipped, (0, 2, 1, 3)).reshape(packs, keys, pack * width)
+    flipped = jnp.pad(flipped, ((0, 0), (0, padded - keys), (0, lanes - pack * width)))
+    mask_low = jnp.transpose(pair_mask).astype(jnp.bfloat16)
+    mask_low = jnp.pad(mask_low, ((0, 0), (0, round_up(rows, 128) - rows)))
+    chunk = 2 if per % 2 == 0 else 1
+    chunks = per // chunk
+    bf16, f32 = jnp.bfloat16, jnp.float32
+    anywhere = pl.BlockSpec(memory_space=pl.ANY)
+    on_chip = pl.BlockSpec(memory_space=pltpu.VMEM)
+    sem = pltpu.SemaphoreType.DMA
+    tile_shape = jax.ShapeDtypeStruct(query_proj.shape, bf16)
+    gq, gk, gv, gb = pl.pallas_call(
+        functools.partial(fused_kernel, rows_n, cols_n, pack),
+        name="triangle_grads",
+        out_shape=(
+            tile_shape, tile_shape, tile_shape,
+            jax.ShapeDtypeStruct((packs, padded, lanes), f32),
+        ),
+        in_specs=[anywhere] * 4 + [on_chip] * 2,
+        out_specs=(anywhere, anywhere, anywhere, on_chip),
+        scratch_shapes=[
+            pltpu.VMEM((4, per, count, channels), bf16),
+            pltpu.VMEM((3, per, count, channels), bf16),
+            pltpu.VMEM((rows_n, cols_n, packs, padded, lanes), bf16),
+            pltpu.VMEM((count, mask_low.shape[1]), bf16),
+            pltpu.VMEM((HEADS, count, count), f32),
+            pltpu.VMEM((HEADS, count, count), f32),
+            pltpu.VMEM((rows_n, HEADS, padded, count), bf16),
+            pltpu.VMEM((rows_n, HEADS, padded, count), bf16),
+            pltpu.VMEM((cols_n, packs, padded, lanes), bf16),
+            pltpu.VMEM((cols_n, packs, padded, lanes), bf16),
+            sem((chunks, cols_n, 4)), sem((chunks, cols_n, 4)),
+            sem((chunks, cols_n, 3)), sem((chunks, cols_n, 3)),
+            sem((cols_n,)), sem((cols_n,)),
+            sem((rows_n,)), sem((rows_n,)),
+            sem((cols_n,)), sem((cols_n,)),
+            sem((rows_n,)), sem((rows_n,)),
+            sem((cols_n,)), sem((cols_n,)),
+            sem((6,)),
+        ],
+        compiler_params=pltpu.CompilerParams(collective_id=0, has_side_effects=True),
+    )(query_proj, key_proj, value_proj, grad_out, flipped, mask_low)
+    gb = gb[:, :keys, :pack * width].reshape(packs, keys, pack, width)
+    gb = jnp.transpose(gb, (0, 2, 3, 1)).reshape(HEADS, width, keys)
+    return gq, gk, gv, gb
+
+
+def choose(rows_n, cols_n):
+    def run(*arrays):
+        count = arrays[0].shape[1] * cols_n
+        if count * count * 4 <= 512 * 1024 and arrays[0].shape[0] % cols_n == 0:
+            return fused(rows_n, cols_n, *arrays)
+        return local(*arrays)
+
+    return run
+
+
 def solution(mesh):
     placed = (
         P("row", "col", None),
@@ -137,7 +458,7 @@
         P("row", "col", None),
     )
     return jax.shard_map(
-        local,
+        choose(mesh.shape["row"], mesh.shape["col"]),
         mesh=mesh,
         in_specs=placed,
         out_specs=(

time: 198 us -> 66.9 us (0.34)
  blocking collectives: 71.3 us -> 0 us
  waiting for transfers between devices: 58.9 us -> 0 us
  Pallas kernels: 0 us -> 58.6 us
  local copies, waits for them, and re-layouts: 26.4 us -> 7.25 us
  starting transfers between devices: 15.8 us -> 0 us
  between operations: 14.2 us -> 0.65 us
  matrix products: 7.33 us -> 0 us
  other arithmetic: 2.1 us -> 0.01 us
    pallas_call x0 -> x1, Pallas kernels: none -> 58.6 us  [fused(): pl.pallas_call(functools.partial(fused_kernel, rows_n, cols_n, pack), nam...]
    all_to_all x4 -> x0, blocking collectives: 46.9 us -> none  [the longest x1 11.8 us: local(): lax.all_to_all(query_proj, 'col', split_axis=0, concat_axis=1, tiled=True)]
    all_to_all x4 -> x0, waiting for transfers between devices: 29.6 us -> none  [the longest x1 17.4 us: local(): lax.all_to_all(grad_values.astype(jnp.bfloat16), 'col', split_axis=1, con...]
    reduce_scatter x1 -> x0, waiting for transfers between devices: 29.2 us -> none  [local(): lax.psum_scatter(bias_part, 'row', scatter_dimension=2, tiled=True)]
    all_gather x2 -> x0, blocking collectives: 24.4 us -> none  [the longest x1 15.1 us: local(): bias_full = lax.all_gather(bias_rows, 'col', axis=1, tiled=True)]
    all_to_all x4 -> x0, starting transfers between devices: 15.7 us -> none  [the longest x1 5.36 us: local(): lax.all_to_all(grad_values.astype(jnp.bfloat16), 'col', split_axis=1, con...]
    dynamic_slice x24 -> x0, local copies, waits for them, and re-layouts: 6.64 us -> none  [all_blocks(): lax.scan(one_block, start_sum, (split_rows(queries), split_rows(keys_all)...]
    dynamic_update_slice x15 -> x0, local copies, waits for them, and re-layouts: 5.14 us -> none  [all_blocks(): lax.scan(one_block, start_sum, (split_rows(queries), split_rows(keys_all)...]
  transfers between devices with their start and end apart: 6 -> 0, of which waited for: 4 -> 0; matrix products, arithmetic and copies ran while one was open for 5% -> 0% of each run, Pallas kernels for 0% -> 0%
where the time goes in v1:
time: 66.9 us; the launch traced here: 66.5 us
  Pallas kernels  58.6 us (88%)
  local copies, waits for them, and re-layouts  7.25 us (11%)
    pallas_call x1, Pallas kernels, fused(): pl.pallas_call(functools.partial(fused_kernel, rows_n, cols_n, pack), nam...  58.6 us
    unnamed x9, local copies, waits for them, and re-layouts  3.62 us

profile of v1, /device:TPU:0, one launch (start us, length us, event | category | flops | bytes accessed | tf_op | source)
XLA Modules:
  0.0 66.5 jit_solution(2955591108632954891)
XLA Ops:
  0.6 0.8 %copy.17 = bf16[2,2,24,48]{3,1,2,0:T(2,128)(2,1)S(1)} copy(bf16[2,2,24,48]{3,2,1,0:T(8,128)(2,1)} %bitcast.13) | data formatting | bytes 18432 | tf_op jit(solution)/shard_map/reshape | solution.py:393
  1.4 0.1 reshape.21
  1.5 0.0 copy-start.2
  1.5 0.6 pad.8.bias_ref
  2.1 0.1 copy-done.2
  2.2 0.1 copy.14
  2.3 0.6 pad.9.mask_ref
  2.9 58.6 %triangle_grads.1 = (bf16[24,48,128]{2,1,0:T(8,128)(2,1)}, bf16[24,48,128]{2,1,0:T(8,128)(2,1)}, bf16[24,48,128]{2,1,0:T(8,128)(2,1)}, f32[2,32,128]{2,1,0:T(8,128)}) custom-call(bf16[24,48,128]{2,1,0:T(8,128)(2,1)} %q_ref.1, bf16[24,48,128]{2,1,0:T(8,128)(2,1)} %k_ref.1, bf16[24,48,128]{2,1,0:T(8,128)(2,1)} %v_ref.1, bf16[24,48,128]{2,1,0:T(8,128)(2,1)} %g_ref.1, ...), custom_call_target="tpu_custom_call" | custom-call | tf_op jit(solution)/shard_map/triangle_grads/pallas_call | solution.py:405
  61.5 0.7 %slice.3 = f32[2,24,96]{2,1,0:T(8,128)S(1)} slice(f32[2,32,128]{2,1,0:T(8,128)} %get-tuple-element.11), slice={[0:2], [0:24], [0:96]} | slice | bytes 36864 | tf_op jit(solution)/shard_map/slice | solution.py:436
  62.3 0.1 reshape.22
  62.4 0.6 copy.15
  63.0 0.0 copy-start.1
  63.0 1.7 %copy.21 = bf16[24,48,128]{2,1,0:T(8,128)(2,1)} copy(bf16[24,48,128]{2,1,0:T(8,128)(2,1)} %get-tuple-element.16) | data formatting | bytes 589824
  64.7 0.0 copy-done.1
  64.7 0.0 copy-start
  64.7 0.7 %copy.22 = bf16[24,48,128]{2,1,0:T(8,128)(2,1)} copy(bf16[24,48,128]{2,1,0:T(8,128)(2,1)S(1)} %copy-done.1) | data formatting | bytes 589824
  65.5 0.4 copy-done
  65.8 0.7 %copy.23 = bf16[24,48,128]{2,1,0:T(8,128)(2,1)} copy(bf16[24,48,128]{2,1,0:T(8,128)(2,1)S(1)} %copy-done) | data formatting | bytes 589824
  (1 shorter events, 0.0 us)
Async XLA Ops:
  1.5 0.7 %copy-start.2 = (s32[24,48]{1,0:T(8,128)S(1)}, s32[24,48]{1,0:T(8,128)}, u32[]{:S(2)}) copy-start(s32[24,48]{1,0:T(8,128)} %param.10) | copy-start | bytes 13828
  63.0 1.7 %copy-start.1 = (bf16[24,48,128]{2,1,0:T(8,128)(2,1)S(1)}, bf16[24,48,128]{2,1,0:T(8,128)(2,1)}, u32[]{:S(2)}) copy-start(bf16[24,48,128]{2,1,0:T(8,128)(2,1)} %get-tuple-element.17) | copy-start | bytes 884740
  64.7 1.1 %copy-start = (bf16[24,48,128]{2,1,0:T(8,128)(2,1)S(1)}, bf16[24,48,128]{2,1,0:T(8,128)(2,1)}, u32[]{:S(2)}) copy-start(bf16[24,48,128]{2,1,0:T(8,128)(2,1)} %get-tuple-element.18) | copy-start | bytes 884740

commit v2 on v1

--- a/solution.py
+++ b/solution.py
@@ -130,6 +130,7 @@
     return (grad_query, grad_key, grad_value, grad_bias)
 
 
+HELD_CHUNKS = 0
 MESH = pl.DeviceIdType.MESH
 
 
@@ -139,9 +140,9 @@
 
 def fused_kernel(
     rows_n, cols_n, pack,
-    q_ref, k_ref, v_ref, g_ref, bias_ref, mask_ref,
+    q_ref, k_ref, v_ref, g_ref, bias_in, mask_in,
     gq_ref, gk_ref, gv_ref, gb_ref,
-    got, stage, bias_all, mask_all, bias_full, bias_sum, part, part_in, tile, tile_in,
+    bias_ref, mask_ref, got, stage, bias_all, mask_all, bias_full, bias_sum, part, part_in, tile, tile_in,
     in_send, in_recv, out_send, out_recv, bc_send, bc_recv, br_send, br_recv,
     mk_send, mk_recv, pr_send, pr_recv, pc_send, pc_recv, own_sem,
 ):
@@ -150,9 +151,11 @@
     count = got.shape[2]
     width = q_ref.shape[1]
     keys = bias_sum.shape[1] // rows_n
+    rows_here = mask_in.shape[0]
     packs, padded, lanes = bias_ref.shape
     chunk = 2 if per % 2 == 0 else 1
     chunks = per // chunk
+    held = min(chunks, HELD_CHUNKS)
     scale = 1.0 / math.sqrt(HEAD_DIM)
     sources = (q_ref, k_ref, v_ref, g_ref)
     results = (gq_ref, gk_ref, gv_ref)
@@ -160,8 +163,18 @@
     def row_peer(d):
         return (lax.rem(row + d, rows_n), col)
 
+    paired = cols_n & (cols_n - 1) == 0
+
     def col_peer(d):
-        return (row, lax.rem(col + d, cols_n))
+        if not paired:
+            return (row, lax.rem(col + d, cols_n))
+        other = 0
+        bit = 1
+        while bit < cols_n:
+            mine = lax.rem(col // bit, 2)
+            other = other + bit * (1 - mine if d & bit else mine)
+            bit = bit * 2
+        return (row, other)
 
     def remote(src, dst, send, recv, peer):
         return pltpu.make_async_remote_copy(
@@ -169,11 +182,34 @@
             device_id=peer, device_id_type=MESH,
         )
 
+    nn = (((1,), (0,)), ((), ()))
+    nt = (((1,), (1,)), ((), ()))
+    tn = (((0,), (0,)), ((), ()))
     barrier = pltpu.get_barrier_semaphore()
     for d in range(1, rows_n):
         pl.semaphore_signal(barrier, inc=1, device_id=row_peer(d), device_id_type=MESH)
     for d in range(1, cols_n):
         pl.semaphore_signal(barrier, inc=1, device_id=col_peer(d), device_id_type=MESH)
+
+    def shifted(shape, shift):
+        at = lax.broadcasted_iota(jnp.int32, shape, 0)
+        lane = lax.broadcasted_iota(jnp.int32, shape, 1)
+        return jnp.where(lane == at + shift, 1.0, 0.0).astype(jnp.bfloat16)
+
+    bias_ref[...] = jnp.zeros_like(bias_ref)
+    for p in range(packs):
+        flipped = jnp.zeros((keys, lanes), jnp.float32)
+        for hh in range(pack):
+            flipped = flipped + lax.dot_general(
+                bias_in[p * pack + hh], shifted((width, lanes), hh * width), nn,
+                preferred_element_type=jnp.float32,
+            )
+        bias_ref[p, 0:keys, :] = flipped.astype(jnp.bfloat16)
+    mask_ref[...] = lax.dot_general(
+        mask_in[...].astype(jnp.float32).astype(jnp.bfloat16),
+        shifted((rows_here, mask_ref.shape[1]), 0), tn,
+        preferred_element_type=jnp.float32,
+    ).astype(jnp.bfloat16)
     pl.semaphore_wait(barrier, rows_n + cols_n - 2)
 
     my_cols = pl.ds(pl.multiple_of(col * width, width), width)
@@ -200,7 +236,7 @@
 
     def in_copies(c):
         copies = []
-        for d in range(1, cols_n):
+        for d in reversed(range(1, cols_n)):
             peer = col_peer(d)
             for a in range(4):
                 copies.append(remote(
@@ -212,7 +248,7 @@
 
     def out_copies(c):
         copies = []
-        for d in range(1, cols_n):
+        for d in reversed(range(1, cols_n)):
             peer = col_peer(d)
             there = pl.ds(pl.multiple_of(peer[1] * width, width), width)
             for a in range(3):
@@ -274,8 +310,6 @@
                     whole[r * padded:r * padded + keys]
                 )
 
-    nt = (((1,), (1,)), ((), ()))
-    tn = (((0,), (0,)), ((), ()))
     channel = lax.broadcasted_iota(jnp.int32, (count, HEADS * HEAD_DIM), 1)
     mask_lane = lax.broadcasted_iota(jnp.int32, mask_all.shape, 1)
 
@@ -322,8 +356,13 @@
         def _(r):
             one_row(c * chunk + r)
 
-        for copy in out_copies(c) + own_outs(c):
+        for copy in own_outs(c):
             copy.start()
+
+        @pl.when(c < chunks - held)
+        def _():
+            for copy in out_copies(c):
+                copy.start()
 
     for r in range(rows_n):
         for h in range(HEADS):
@@ -361,12 +400,20 @@
         ))
     for copy in part_col:
         copy.start()
+
+    @pl.loop(chunks - held, chunks)
+    def _(c):
+        for copy in out_copies(c):
+            copy.start()
+
     for copy in part_col:
         copy.wait_recv()
     total = tile[col].astype(jnp.float32)
     for d in range(1, cols_n):
         total = total + tile_in[lax.rem(col + d, cols_n)].astype(jnp.float32)
-    gb_ref[...] = total
+    for p in range(packs):
+        for hh in range(pack):
+            gb_ref[p * pack + hh] = total[p, 0:keys, hh * width:(hh + 1) * width]
 
     @pl.loop(0, chunks)
     def _(c):
@@ -390,32 +437,30 @@
         pack = pack * 2
     packs = HEADS // pack
     padded, lanes = round_up(keys, 16), round_up(pack * width, 128)
-    flipped = jnp.transpose(pair_bias, (0, 2, 1)).reshape(packs, pack, keys, width)
-    flipped = jnp.transpose(flipped, (0, 2, 1, 3)).reshape(packs, keys, pack * width)
-    flipped = jnp.pad(flipped, ((0, 0), (0, padded - keys), (0, lanes - pack * width)))
-    mask_low = jnp.transpose(pair_mask).astype(jnp.bfloat16)
-    mask_low = jnp.pad(mask_low, ((0, 0), (0, round_up(rows, 128) - rows)))
+    mask_lanes = round_up(rows, 128)
     chunk = 2 if per % 2 == 0 else 1
     chunks = per // chunk
     bf16, f32 = jnp.bfloat16, jnp.float32
     anywhere = pl.BlockSpec(memory_space=pl.ANY)
     on_chip = pl.BlockSpec(memory_space=pltpu.VMEM)
     sem = pltpu.SemaphoreType.DMA
-    tile_shape = jax.ShapeDtypeStruct(query_proj.shape, bf16)
+    tile_shape = pltpu.VMEM(query_proj.shape, bf16)
     gq, gk, gv, gb = pl.pallas_call(
         functools.partial(fused_kernel, rows_n, cols_n, pack),
         name="triangle_grads",
         out_shape=(
             tile_shape, tile_shape, tile_shape,
-            jax.ShapeDtypeStruct((packs, padded, lanes), f32),
+            jax.ShapeDtypeStruct((HEADS, keys, width), f32),
         ),
         in_specs=[anywhere] * 4 + [on_chip] * 2,
-        out_specs=(anywhere, anywhere, anywhere, on_chip),
+        out_specs=(on_chip,) * 4,
         scratch_shapes=[
+            pltpu.VMEM((packs, padded, lanes), bf16),
+            pltpu.VMEM((width, mask_lanes), bf16),
             pltpu.VMEM((4, per, count, channels), bf16),
             pltpu.VMEM((3, per, count, channels), bf16),
             pltpu.VMEM((rows_n, cols_n, packs, padded, lanes), bf16),
-            pltpu.VMEM((count, mask_low.shape[1]), bf16),
+            pltpu.VMEM((count, mask_lanes), bf16),
             pltpu.VMEM((HEADS, count, count), f32),
             pltpu.VMEM((HEADS, count, count), f32),
             pltpu.VMEM((rows_n, HEADS, padded, count), bf16),
@@ -432,10 +477,8 @@
             sem((6,)),
         ],
         compiler_params=pltpu.CompilerParams(collective_id=0, has_side_effects=True),
-    )(query_proj, key_proj, value_proj, grad_out, flipped, mask_low)
-    gb = gb[:, :keys, :pack * width].reshape(packs, keys, pack, width)
-    gb = jnp.transpose(gb, (0, 2, 3, 1)).reshape(HEADS, width, keys)
-    return gq, gk, gv, gb
+    )(query_proj, key_proj, value_proj, grad_out, jnp.transpose(pair_bias, (0, 2, 1)), pair_mask)
+    return gq, gk, gv, jnp.transpose(gb, (0, 2, 1))
 
 
 def choose(rows_n, cols_n):

time: 66.9 us -> 62.8 us (0.939)
  local copies, waits for them, and re-layouts: 7.25 us -> 2.85 us
    pad x2 -> x0, local copies, waits for them, and re-layouts: 1.23 us -> none  [the longest x1 0.61 us: fused(): jnp.pad(flipped, ((0, 0), (0, padded - keys), (0, lanes - pack * width)))]
    reshape x3 -> x0, local copies, waits for them, and re-layouts: 0.94 us -> none  [the longest x1 0.76 us: fused(): jnp.transpose(pair_bias, (0, 2, 1)).reshape(packs, pack, keys, width)]
    unnamed x9 -> x6, local copies, waits for them, and re-layouts: 3.62 us -> 2.85 us
    slice x1 -> x0, local copies, waits for them, and re-layouts: 0.74 us -> none  [fused(): gb = gb[:, :keys, :pack * width].reshape(packs, keys, pack, width)]
where the time goes in v2:
time: 62.8 us; the launch traced here: 62.6 us
  Pallas kernels  59.1 us (94%)
  local copies, waits for them, and re-layouts  2.85 us (5%)
  between operations  0.64 us (1%)
    pallas_call x1, Pallas kernels, fused(): pl.pallas_call(functools.partial(fused_kernel, rows_n, cols_n, pack), nam...  59.1 us
    unnamed x6, local copies, waits for them, and re-layouts  2.85 us

profile of v2, /device:TPU:0, one launch (start us, length us, event | category | flops | bytes accessed | tf_op | source)
XLA Modules:
  0.0 62.6 jit_solution(4399110090271117301)
XLA Ops:
  0.6 59.1 %triangle_grads.1 = (bf16[24,48,128]{2,1,0:T(8,128)(2,1)S(1)}, bf16[24,48,128]{2,1,0:T(8,128)(2,1)S(1)}, bf16[24,48,128]{2,1,0:T(8,128)(2,1)S(1)}, f32[4,24,48]{2,1,0:T(8,128)}) custom-call(bf16[24,48,128]{2,1,0:T(8,128)(2,1)} %q_ref.1, bf16[24,48,128]{2,1,0:T(8,128)(2,1)} %k_ref.1, bf16[24,48,128]{2,1,0:T(8,128)(2,1)} %v_ref.1, bf16[24,48,128]{2,1,0:T(8,128)(2,1)} %g_ref.1, ...), custom_call_target="tpu_custom_call" | custom-call | tf_op jit(solution)/shard_map/triangle_grads/pallas_call | solution.py:448
  59.7 0.7 %copy.14 = bf16[24,48,128]{2,1,0:T(8,128)(2,1)} copy(bf16[24,48,128]{2,1,0:T(8,128)(2,1)S(1)} %get-tuple-element.12) | data formatting | bytes 589824
  60.5 0.7 %copy.15 = bf16[24,48,128]{2,1,0:T(8,128)(2,1)} copy(bf16[24,48,128]{2,1,0:T(8,128)(2,1)S(1)} %get-tuple-element.13) | data formatting | bytes 589824
  61.2 0.0 copy-start
  61.2 0.7 %copy.16 = bf16[24,48,128]{2,1,0:T(8,128)(2,1)} copy(bf16[24,48,128]{2,1,0:T(8,128)(2,1)S(1)} %get-tuple-element.14) | data formatting | bytes 589824
  61.9 0.1 copy-done
  62.0 0.6 copy.17
Async XLA Ops:
  61.2 0.8 %copy-start = (f32[4,24,48]{2,1,0:T(8,128)S(1)}, f32[4,24,48]{2,1,0:T(8,128)}, u32[]{:S(2)}) copy-start(f32[4,24,48]{2,1,0:T(8,128)} %get-tuple-element.11) | copy-start | bytes 55300
